TPU v7x, 256 devices: a whole 4x4x8 slice. The times are simulated.
256 devices in a mesh: trial: 2 (over core), qa: 16 (over y, x), qb: 8 (over z).
Axes of the slice: x: 4, y: 4, z: 8, core: 2. Of those that a mesh axis runs over, the one named last changes fastest.
Arguments:
- wave_parts: float32 [4, 512, 128, 128], P('trial', ('qa', 'qb')), parts along dimension 0, may hold values from -6 to 6
- level_table: float32 [1024, 128, 128], P(('trial', 'qa', 'qb')), parts along dimension 0, may hold values from -2 to 2
- diagonal_angles: float32 [6, 128], P('trial'), parts along dimension 0, may hold values from 0.3 to 1.2
- turn_angles: float32 [6, 4], P('trial'), parts along dimension 0, may hold values from 0.3 to 1.2
Outputs:
- final_parts: float32 [4, 512, 128, 128], P('trial', ('qa', 'qb')), parts along dimension 0
There are 2 independent parts, one for each index of `trial`. A program takes and returns all parts, laid end to end along the dimension named above; each array names one. Nothing has to cross between parts.
All inputs are finite; a program needn't handle non-finite values.
Results may differ from a plain program's by a relative error of at most 0.0003.
Values sent between devices are 32-bit elements.
A program may use at most 64 MiB of HBM per device.

v0:
```python
import functools

import jax
import jax.numpy as jnp
from jax import lax
from jax.experimental import pallas as pl
from jax.experimental.pallas import tpu as pltpu
from jax.sharding import PartitionSpec as P

LAYERS = 3


def count_bits(values, count):
    places = jnp.arange(count.bit_length() - 1, dtype=jnp.int32)
    return jnp.sum(values[..., None] >> places & 1, axis=-1)


def rotation_table(count, angle):
    rank = jnp.arange(count, dtype=jnp.int32)
    apart = count_bits(rank[:, None] ^ rank[None, :], count)
    bits = count.bit_length() - 1
    size = jnp.cos(angle) ** (bits - apart).astype(jnp.float32) * jnp.sin(angle) ** apart.astype(
        jnp.float32
    )
    real_sign = jnp.where(apart % 4 == 0, 1.0, jnp.where(apart % 4 == 2, -1.0, 0.0)).astype(
        jnp.float32
    )
    imag_sign = jnp.where(apart % 4 == 1, -1.0, jnp.where(apart % 4 == 3, 1.0, 0.0)).astype(
        jnp.float32
    )
    return (size * real_sign, size * imag_sign)


def mix_dim(values, dim, angle):
    real_part, imag_part = rotation_table(values.shape[dim], angle)

    def times(table):
        moved = jnp.tensordot(values, table, axes=([dim], [0]), precision=lax.Precision.HIGHEST)
        return jnp.moveaxis(moved, -1, dim)

    by_real = times(real_part)
    by_imag = times(imag_part)
    return jnp.stack([by_real[0] - by_imag[1], by_real[1] + by_imag[0]])


def phase_step(values, levels, angle):
    turn = angle * levels
    return jnp.stack(
        [
            values[0] * jnp.cos(turn) + values[1] * jnp.sin(turn),
            values[1] * jnp.cos(turn) - values[0] * jnp.sin(turn),
        ]
    )


def cos_sin(turn):
    half = 0.5 * turn
    y = half * half
    sine = -1 / 39916800
    for term in (1 / 362880, -1 / 5040, 1 / 120, -1 / 6, 1.0):
        sine = sine * y + term
    sine = sine * half
    cosine = 1 / 479001600
    for term in (-1 / 3628800, 1 / 40320, -1 / 720, 1 / 24, -0.5, 1.0):
        cosine = cosine * y + term
    return 1.0 - 2.0 * sine * sine, 2.0 * sine * cosine


def split(x):
    high = x.astype(jnp.bfloat16)
    return high, (x - high.astype(jnp.float32)).astype(jnp.bfloat16)


def dot(a, b):
    return jnp.dot(a, b, preferred_element_type=jnp.float32)


def right_weights(table):
    high, low = split(table)
    return jnp.concatenate(
        [jnp.concatenate([high, low], 1), jnp.concatenate([high, jnp.zeros_like(low)], 1)], 0)


def left_weights(table):
    high, low = split(table)
    return jnp.concatenate(
        [jnp.concatenate([high, high], 1), jnp.concatenate([low, jnp.zeros_like(low)], 1)], 0)


def times_right(x, weights):
    both = dot(jnp.concatenate(split(x), 1), weights)
    size = both.shape[1] // 2
    return both[:, :size] + both[:, size:]


def times_left(weights, x):
    both = dot(weights, jnp.concatenate(split(x), 0))
    size = both.shape[0] // 2
    return both[:size] + both[size:]


def moved_bits(fields, order):
    def places(names):
        at, low = {}, 0
        for name in reversed(names):
            at[name] = low
            low += fields[name][0]
        return at

    into, out = places(order[0]), places(order[1])
    return [
        (out[name] + i, into[name] + i, group)
        for name, (bits, group) in fields.items()
        for i in range(bits)
    ]


def turn_table(size, bits, angles, out_axis):
    out = lax.broadcasted_iota(jnp.int32, (size, size), out_axis)
    into = lax.broadcasted_iota(jnp.int32, (size, size), 1 - out_axis)
    table = None
    for out_at, in_at, group in bits:
        o = (out >> out_at) & 1
        i = (into >> in_at) & 1
        if group is None:
            factor = jnp.where(o == i, 1.0, 0.0)
        else:
            c, s = angles[group]
            factor = jnp.where(o == i, c, jnp.where(o > i, -s, s))
        table = factor if table is None else table * factor
    return table


def mix_list(xs, groups, angles):
    xs = list(xs)
    step = len(xs)
    for group in groups:
        c, s = angles[group]
        step //= 2
        for j in range(len(xs)):
            if not j & step:
                u, v = xs[j], xs[j + step]
                xs[j], xs[j + step] = c * u + s * v, c * v - s * u
    return xs


def log2(count):
    return count.bit_length() - 1


def kernel(na, nb, wave_hbm, level_hbm, diag_hbm, turns_hbm, out, wave, level, diag, turns, in_sem, x1, s1, r1, x2, s2, r2, x3, s3, r3,
           tb, tp, tc, cs, tables, send_sem, recv_sem, own_sem):
    n = na * nb
    blocks, rows, lanes = wave_hbm.shape[1:]
    high = n // blocks
    rest = rows // high
    low = rest // n
    f32 = jnp.float32
    a = lax.axis_index("qa")
    b = lax.axis_index("qb")
    me = a * nb + b

    def flipped(x, mask):
        for i in range(log2(n)):
            if mask >> i & 1:
                x = x + (1 << i) * (1 - 2 * lax.rem(lax.div(x, 1 << i), 2))
        return x

    def where_is(k):
        pa, pb = flipped(a, k // nb), flipped(b, k % nb)
        return pa * nb + pb, {"qa": pa, "qb": pb}

    masks = sorted(range(1, n), key=lambda k: (-(k % nb), -(k // nb)))

    fetched = [
        pltpu.make_async_copy(src, dst, in_sem.at[i])
        for i, (src, dst) in enumerate(
            ((turns_hbm, turns), (level_hbm, level), (diag_hbm, diag), (wave_hbm, wave)))
    ]
    for copy in fetched:
        copy.start()

    barrier = pltpu.get_barrier_semaphore()

    for k in masks:
        pl.semaphore_signal(barrier, inc=1, device_id=where_is(k)[1], device_id_type=pl.DeviceIdType.MESH)

    def remote(src, dst, which, k):
        peer, to = where_is(k)
        return pltpu.make_async_remote_copy(
            src_ref=src(peer), dst_ref=dst(me), send_sem=send_sem.at[which, k],
            recv_sem=recv_sem.at[which, k], device_id=to, device_id_type=pl.DeviceIdType.MESH)

    def send(src, dst, which):
        for k in masks:
            remote(src, dst, which, k).start()
        pltpu.make_async_copy(src(me), dst(me), own_sem.at[which]).start()

    def arrive(src, dst, which):
        for k in masks:
            remote(src, dst, which, k).wait_recv()
        pltpu.make_async_copy(src(me), dst(me), own_sem.at[which]).wait()

    def sent(src, dst, which):
        for k in masks:
            remote(src, dst, which, k).wait_send()

    plans = []
    for p in range(2):
        plans.append((lambda i, p=p: s1.at[p, i], lambda i, p=p: r1.at[p, i], p))
    for p in range(2):
        plans.append((lambda i, p=p: s2.at[p, :, i], lambda i, p=p: r2.at[p, i], 2 + p))
    for p in range(2):
        plans.append((lambda i, p=p: s3.at[p, i], lambda i, p=p: r3.at[p, i], 4 + p))
    per = n // blocks
    table_b = (lambda i: level.at[i // per, pl.ds(pl.multiple_of((i % per) * rest, 8), rest)], lambda i: tb.at[i], 6)
    table_c = (lambda i: tp.at[:, i], lambda i: tc.at[i], 7)

    fetched[0].wait()
    angles = []
    for layer in range(LAYERS):
        angles.append([cos_sin(jnp.full((1, lanes), turns[layer, g], f32)) for g in range(4)])
    lane_bits = [(i, i, 0) for i in range(log2(lanes))]

    fields_b = dict(b=(log2(nb), 3), mid=(log2(n), 1), low=(log2(low), 1))
    bits_b = moved_bits(fields_b, (("b", "mid", "low"), ("mid", "b", "low")))
    fields_c = dict(block=(log2(blocks), 2), high=(log2(high), 1), b=(log2(nb), 3), low=(log2(low), 1))
    bits_c = moved_bits(fields_c, (("block", "high", "b", "low"), ("b", "block", "high", "low")))
    fields_a = dict(mid=(log2(n), 1), high=(log2(high), None), low=(log2(low), None))
    bits_a = moved_bits(fields_a, (("mid", "high", "low"), ("high", "mid", "low")))
    row_bits = [[(i, i, 1) for i in range(log2(rows))], bits_b, bits_c]

    def make_tables(layer):
        tables[2 * layer] = right_weights(turn_table(lanes, lane_bits, angles[layer], 1))
        tables[2 * layer + 1] = left_weights(turn_table(rows, row_bits[layer], angles[layer], 0))

    row_at = lax.broadcasted_iota(jnp.int32, (rows, lanes), 0)
    lane_at = lax.broadcasted_iota(jnp.int32, (rows, lanes), 1)
    ones = jnp.zeros((rows, lanes), jnp.int32)
    for i in range(log2(rows)):
        ones = ones + ((row_at >> i) & 1)
    for i in range(log2(lanes)):
        ones = ones + ((lane_at >> i) & 1)
    for i in range(log2(n)):
        ones = ones + lax.rem(lax.div(me, 1 << i), 2)

    def power(block):
        q = (ones + block.bit_count()) & 3
        real = jnp.where(q == 0, 1.0, jnp.where(q == 2, -1.0, 0.0))
        imag = jnp.where(q == 1, -1.0, jnp.where(q == 3, 1.0, 0.0))
        return real, imag

    make_tables(0)
    fetched[1].wait()
    pl.semaphore_wait(barrier, n - 1)
    send(*table_b)

    fetched[2].wait()
    fetched[3].wait()
    for g in range(blocks):
        c, s = cos_sin(diag[0:1, :] * level[g])
        re, im = wave[0, g], wave[1, g]
        re, im = re * c + im * s, im * c - re * s
        fr, fi = power(g)
        x1[0, g] = re * fr - im * fi
        x1[1, g] = im * fr + re * fi

    def segment(layer, take, put, plan):
        for p in range(2):
            x = jnp.concatenate([take(p, g) for g in range(blocks)], 0)
            x = times_right(x, tables[2 * layer])
            x = jnp.concatenate([x[g * rows : (g + 1) * rows] for g in range(blocks)], 1)
            x = times_left(tables[2 * layer + 1], x)
            xs = [x[:, g * lanes : (g + 1) * lanes] for g in range(blocks)]
            for g, x in enumerate(mix_list(xs, [2] * log2(blocks), angles[layer])):
                put(p, g, x)
            send(*plan[p])

    def join(received, table, layer, groups, take, put, plan, count):
        def phase(j, carry):
            c, s = cos_sin(diag[layer + 1 : layer + 2, :] * take(table, j))
            cs[0, j] = c
            cs[1, j] = s
            return carry

        lax.fori_loop(0, count, phase, 0)
        make_tables(layer + 1)
        arrive(*plan[0])
        if layer == 0:
            send(*table_c)
        arrive(*plan[1])

        def step(j, carry):
            re = mix_list(take(received.at[0], j), groups, angles[layer])
            im = mix_list(take(received.at[1], j), groups, angles[layer])
            for i in range(n):
                c, s = cs[0, j, i], cs[1, j, i]
                put(0, i, j, re[i] * c + im[i] * s)
                put(1, i, j, im[i] * c - re[i] * s)
            return carry

        lax.fori_loop(0, count, step, 0)

    def put1(p, g, x):
        s1[p, g * per : (g + 1) * per] = x.reshape(per, rest, lanes)

    segment(0, lambda p, g: x1[p, g], put1, plans[0:2])

    arrive(*table_b)
    place = turn_table(rows, [(o, i, None) for o, i, _ in bits_b], None, 0).astype(jnp.bfloat16)
    x = jnp.concatenate([tb[g * nb : (g + 1) * nb].reshape(rows, lanes) for g in range(na)], 1)
    first = x.astype(jnp.bfloat16)
    x = x - first.astype(f32)
    second = x.astype(jnp.bfloat16)
    third = (x - second.astype(f32)).astype(jnp.bfloat16)
    x = dot(place, first) + dot(place, second) + dot(place, third)
    for g in range(na):
        tp[g] = x[:, g * lanes : (g + 1) * lanes].reshape(n, nb * low, lanes)
    def take_b(ref, j):
        return ref[:, pl.ds(pl.multiple_of(j * 8, 8), 8), :]

    def put_b(p, i, j, x):
        x2[p, i, pl.ds(pl.multiple_of(j * 8, 8), 8), :] = x

    join(r1, tb, 0, [2] * log2(na) + [3] * log2(nb), take_b, put_b, plans[0:2], rest // 8)

    def put2(p, g, x):
        s2[p, g] = x.reshape(n, nb * low, lanes)

    segment(1, lambda p, g: x2[p, g * nb : (g + 1) * nb].reshape(rows, lanes), put2, plans[2:4])

    arrive(*table_c)

    def put_c(p, i, j, x):
        x3[p, i, j] = x

    join(r2, tc, 1, [2] * log2(blocks) + [1] * log2(high), lambda ref, j: ref[:, j], put_c, plans[2:4], na)

    def put3(p, g, x):
        s3[p, g * nb : (g + 1) * nb] = x.reshape(nb, blocks, high * low, lanes)

    segment(2, lambda p, g: x3[p, :, g].reshape(rows, lanes), put3, plans[4:6])

    tables[0] = left_weights(turn_table(rows, bits_a, angles[2], 0))
    parts = []
    for p in range(2):
        arrive(*plans[4 + p])
        x = jnp.concatenate([r3[p, :, g].reshape(rows, lanes) for g in range(blocks)], 1)
        parts.append(times_left(tables[0], x))
    for g in range(blocks):
        re, im = [x[:, g * lanes : (g + 1) * lanes] for x in parts]
        fr, fi = power(g)
        out[0, g] = re * fr + im * fi
        out[1, g] = im * fr - re * fi
    for plan in plans + [table_b, table_c]:
        sent(*plan)


def fits(na, nb, blocks, rows, lanes):
    n = na * nb
    if blocks != na or rows != lanes or n % blocks or rows * blocks % (n * n):
        return False
    high = n // blocks
    low = rows // high // n
    return nb * low == 8 and high * low == 8


def fused(wave_parts, level_table, diagonal_angles, turn_angles, na, nb):
    n = na * nb
    _, blocks, rows, lanes = wave_parts.shape
    rest = rows * blocks // n
    f32 = jnp.float32
    V = pltpu.VMEM
    flat = V((2, n, rest, lanes), f32)
    tiles = V((2, n, na, 8, lanes), f32)
    vmem = pl.BlockSpec(memory_space=pltpu.VMEM)
    return pl.pallas_call(
        functools.partial(kernel, na, nb),
        out_shape=jax.ShapeDtypeStruct(wave_parts.shape, f32),
        in_specs=[pl.BlockSpec(memory_space=pltpu.HBM)] * 4,
        out_specs=vmem,
        scratch_shapes=[
            V(wave_parts.shape, f32), V(level_table.shape, f32), V(diagonal_angles.shape, f32),
            pltpu.SMEM(turn_angles.shape, f32), pltpu.SemaphoreType.DMA((4,)),
            V(wave_parts.shape, f32), flat, flat,
            flat, V((2, na, n, 8, lanes), f32), tiles,
            tiles, V((2, n, blocks, 8, lanes), f32), V((2, n, blocks, 8, lanes), f32),
            V((n, rest, lanes), f32), V((na, n, 8, lanes), f32), V((n, na, 8, lanes), f32),
            V((2, na, n, 8, lanes), f32), V((2 * LAYERS, 2 * rows, 2 * lanes), jnp.bfloat16),
            pltpu.SemaphoreType.DMA((8, n)), pltpu.SemaphoreType.DMA((8, n)), pltpu.SemaphoreType.DMA((8,)),
        ],
        compiler_params=pltpu.CompilerParams(
            collective_id=0, has_side_effects=True, vmem_limit_bytes=32 * 1024 * 1024),
    )(wave_parts, level_table, diagonal_angles, turn_angles)


def shards(wave_parts, level_table, diagonal_angles, turn_angles):
    values = wave_parts
    for layer in range(LAYERS):
        values = phase_step(values, level_table, diagonal_angles[layer])
        values = mix_dim(values, 3, turn_angles[layer, 0])
        values = mix_dim(values, 2, turn_angles[layer, 1])
        moved = lax.all_to_all(values, "qa", split_axis=2, concat_axis=1, tiled=True)
        moved = mix_dim(moved, 1, turn_angles[layer, 2])
        values = lax.all_to_all(moved, "qa", split_axis=1, concat_axis=2, tiled=True)
        moved = lax.all_to_all(values, "qb", split_axis=3, concat_axis=1, tiled=True)
        spread = moved.reshape(2, lax.axis_size("qb"), -1, moved.shape[2], moved.shape[3])
        moved = mix_dim(spread, 1, turn_angles[layer, 3]).reshape(moved.shape)
        values = lax.all_to_all(moved, "qb", split_axis=1, concat_axis=3, tiled=True)
    return values


def solution(mesh):
    na, nb = mesh.shape["qa"], mesh.shape["qb"]

    def each(wave_parts, level_table, diagonal_angles, turn_angles):
        args = (wave_parts, level_table, diagonal_angles, turn_angles)
        if fits(na, nb, *wave_parts.shape[1:]):
            return fused(*args, na, nb)
        return shards(*args)

    placed = (
        P("trial", ("qa", "qb"), None, None),
        P(("trial", "qa", "qb"), None, None),
        P("trial", None),
        P("trial", None),
    )
    return jax.shard_map(
        each,
        mesh=mesh,
        in_specs=placed,
        out_specs=P("trial", ("qa", "qb"), None, None),
        check_vma=False,
    )
```

profile of v0, /device:TPU:8, one launch (start us, length us, event | category | flops | bytes accessed | tf_op | source)
XLA Modules:
  0.0 243.2 jit_solution(5712961371041318198)
XLA Ops:
  0.0 1.8 fusion.327
  3.8 2.0 fusion.19
  9.0 1.1 convolution_bitcast_fusion.17
  12.3 7.4 %all-to-all-start = ((f32[2,4,128,128]{3,1,0,2:T(4,128)}), f32[2,4,128,128]{3,1,0,2:T(4,128)S(1)}, u32[]{:S(2)}, u32[]{:S(2)}) async-start(f32[2,4,128,128]{3,1,0,2:T(4,128)} %copy.169), calls=%async_computation | async-start | bytes 1048576 | tf_op jit(solution)/shard_map/all_to_all | solution.py:403
  21.2 7.6 %all-to-all-done = f32[2,4,128,128]{3,1,0,2:T(4,128)S(1)} async-done(((f32[2,4,128,128]{3,1,0,2:T(4,128)}), f32[2,4,128,128]{3,1,0,2:T(4,128)S(1)}, u32[]{:S(2)}, u32[]{:S(2)}) %all-to-all-start) | async-done | bytes 524320 | tf_op jit(solution)/shard_map/all_to_all | solution.py:403
  31.1 14.1 %all_to_all.201 = f32[2,64,8,128]{3,2,0,1:T(8,128)S(1)} all-to-all(f32[2,64,8,128]{3,2,0,1:T(8,128)S(1)} %copy.174), channel_id=1, replica_groups=mesh['trial'=2,'qa'=16,'qb'=8] {'qa'}, dimensions={1} | all-to-all | bytes 1048576 | tf_op jit(solution)/shard_map/all_to_all | solution.py:405
  46.3 8.5 %all-to-all-start.2 = ((f32[2,4,128,128]{2,1,0,3:T(4,128)}), f32[2,4,128,128]{2,1,0,3:T(4,128)S(1)}, u32[]{:S(2)}, u32[]{:S(2)}) async-start(f32[2,4,128,128]{2,1,0,3:T(4,128)} %copy.177), calls=%async_computation.2 | async-start | bytes 1048576 | tf_op jit(solution)/shard_map/all_to_all | solution.py:406
  56.2 13.1 %all-to-all-done.2 = f32[2,4,128,128]{2,1,0,3:T(4,128)S(1)} async-done(((f32[2,4,128,128]{2,1,0,3:T(4,128)}), f32[2,4,128,128]{2,1,0,3:T(4,128)S(1)}, u32[]{:S(2)}, u32[]{:S(2)}) %all-to-all-start.2) | async-done | bytes 524320 | tf_op jit(solution)/shard_map/all_to_all | solution.py:406
  72.2 3.8 %all-to-all-start.3 = ((f32[2,32,128,16]{2,3,0,1:T(8,128)}), f32[2,32,128,16]{2,3,0,1:T(8,128)S(1)}, u32[]{:S(2)}, u32[]{:S(2)}) async-start(f32[2,32,128,16]{2,3,0,1:T(8,128)} %copy.184), calls=%async_computation.3 | async-start | bytes 1048576 | tf_op jit(solution)/shard_map/all_to_all | solution.py:409
  78.7 14.1 %all-to-all-done.3 = f32[2,32,128,16]{2,3,0,1:T(8,128)S(1)} async-done(((f32[2,32,128,16]{2,3,0,1:T(8,128)}), f32[2,32,128,16]{2,3,0,1:T(8,128)S(1)}, u32[]{:S(2)}, u32[]{:S(2)}) %all-to-all-start.3) | async-done | bytes 524320 | tf_op jit(solution)/shard_map/all_to_all | solution.py:409
  100.0 6.2 %all-to-all-start.4 = ((f32[2,4,128,128]{3,1,0,2:T(4,128)}), f32[2,4,128,128]{3,1,0,2:T(4,128)S(1)}, u32[]{:S(2)}, u32[]{:S(2)}) async-start(f32[2,4,128,128]{3,1,0,2:T(4,128)} %copy.194), calls=%async_computation.4 | async-start | bytes 1048576 | tf_op jit(solution)/shard_map/all_to_all | solution.py:403
  107.6 6.3 %all-to-all-done.4 = f32[2,4,128,128]{3,1,0,2:T(4,128)S(1)} async-done(((f32[2,4,128,128]{3,1,0,2:T(4,128)}), f32[2,4,128,128]{3,1,0,2:T(4,128)S(1)}, u32[]{:S(2)}, u32[]{:S(2)}) %all-to-all-start.4) | async-done | bytes 524320 | tf_op jit(solution)/shard_map/all_to_all | solution.py:403
  116.3 12.8 %all_to_all.202 = f32[2,64,8,128]{3,2,0,1:T(8,128)S(1)} all-to-all(f32[2,64,8,128]{3,2,0,1:T(8,128)S(1)} %copy.199), channel_id=1, replica_groups=mesh['trial'=2,'qa'=16,'qb'=8] {'qa'}, dimensions={1} | all-to-all | bytes 1048576 | tf_op jit(solution)/shard_map/all_to_all | solution.py:405
  130.1 3.5 %all-to-all-start.6 = ((f32[2,4,128,128]{2,1,0,3:T(4,128)}), f32[2,4,128,128]{2,1,0,3:T(4,128)S(1)}, u32[]{:S(2)}, u32[]{:S(2)}) async-start(f32[2,4,128,128]{2,1,0,3:T(4,128)} %copy.202), calls=%async_computation.6 | async-start | bytes 1048576 | tf_op jit(solution)/shard_map/all_to_all | solution.py:406
  134.9 14.5 %all-to-all-done.6 = f32[2,4,128,128]{2,1,0,3:T(4,128)S(1)} async-done(((f32[2,4,128,128]{2,1,0,3:T(4,128)}), f32[2,4,128,128]{2,1,0,3:T(4,128)S(1)}, u32[]{:S(2)}, u32[]{:S(2)}) %all-to-all-start.6) | async-done | bytes 524320 | tf_op jit(solution)/shard_map/all_to_all | solution.py:406
  152.2 3.7 %all-to-all-start.7 = ((f32[2,32,128,16]{2,3,0,1:T(8,128)}), f32[2,32,128,16]{2,3,0,1:T(8,128)S(1)}, u32[]{:S(2)}, u32[]{:S(2)}) async-start(f32[2,32,128,16]{2,3,0,1:T(8,128)} %copy.209), calls=%async_computation.7 | async-start | bytes 1048576 | tf_op jit(solution)/shard_map/all_to_all | solution.py:409
  158.9 10.8 %all-to-all-done.7 = f32[2,32,128,16]{2,3,0,1:T(8,128)S(1)} async-done(((f32[2,32,128,16]{2,3,0,1:T(8,128)}), f32[2,32,128,16]{2,3,0,1:T(8,128)S(1)}, u32[]{:S(2)}, u32[]{:S(2)}) %all-to-all-start.7) | async-done | bytes 524320 | tf_op jit(solution)/shard_map/all_to_all | solution.py:409
  172.8 1.1 convolution_bitcast_fusion.5
  176.1 7.5 %all-to-all-start.8 = ((f32[2,4,128,128]{3,1,0,2:T(4,128)}), f32[2,4,128,128]{3,1,0,2:T(4,128)S(1)}, u32[]{:S(2)}, u32[]{:S(2)}) async-start(f32[2,4,128,128]{3,1,0,2:T(4,128)} %copy.219), calls=%async_computation.8 | async-start | bytes 1048576 | tf_op jit(solution)/shard_map/all_to_all | solution.py:403
  185.0 6.3 %all-to-all-done.8 = f32[2,4,128,128]{3,1,0,2:T(4,128)S(1)} async-done(((f32[2,4,128,128]{3,1,0,2:T(4,128)}), f32[2,4,128,128]{3,1,0,2:T(4,128)S(1)}, u32[]{:S(2)}, u32[]{:S(2)}) %all-to-all-start.8) | async-done | bytes 524320 | tf_op jit(solution)/shard_map/all_to_all | solution.py:403
  193.6 12.7 %all_to_all.203 = f32[2,64,8,128]{3,2,0,1:T(8,128)S(1)} all-to-all(f32[2,64,8,128]{3,2,0,1:T(8,128)S(1)} %copy.224), channel_id=1, replica_groups=mesh['trial'=2,'qa'=16,'qb'=8] {'qa'}, dimensions={1} | all-to-all | bytes 1048576 | tf_op jit(solution)/shard_map/all_to_all | solution.py:405
  207.4 3.5 %all-to-all-start.10 = ((f32[2,4,128,128]{2,1,0,3:T(4,128)}), f32[2,4,128,128]{2,1,0,3:T(4,128)S(1)}, u32[]{:S(2)}, u32[]{:S(2)}) async-start(f32[2,4,128,128]{2,1,0,3:T(4,128)} %copy.227), calls=%async_computation.10 | async-start | bytes 1048576 | tf_op jit(solution)/shard_map/all_to_all | solution.py:406
  212.4 12.2 %all-to-all-done.10 = f32[2,4,128,128]{2,1,0,3:T(4,128)S(1)} async-done(((f32[2,4,128,128]{2,1,0,3:T(4,128)}), f32[2,4,128,128]{2,1,0,3:T(4,128)S(1)}, u32[]{:S(2)}, u32[]{:S(2)}) %all-to-all-start.10) | async-done | bytes 524320 | tf_op jit(solution)/shard_map/all_to_all | solution.py:406
  226.7 15.5 %all_to_all.204 = f32[2,32,128,16]{2,3,0,1:T(8,128)S(1)} all-to-all(f32[2,32,128,16]{2,3,0,1:T(8,128)S(1)} %copy.234), channel_id=1, replica_groups=mesh['trial'=2,'qa'=16,'qb'=8] {'qb'}, dimensions={1} | all-to-all | bytes 1048576 | tf_op jit(solution)/shard_map/all_to_all | solution.py:409
  (97 shorter events, 35.5 us)
Async XLA Ops:
  3.1 0.7 copy-start.1
  12.3 16.5 %all-to-all-start = ((f32[2,4,128,128]{3,1,0,2:T(4,128)}), f32[2,4,128,128]{3,1,0,2:T(4,128)S(1)}, u32[]{:S(2)}, u32[]{:S(2)}) async-start(f32[2,4,128,128]{3,1,0,2:T(4,128)} %copy.169), calls=%async_computation | async-start | bytes 1048576 | tf_op jit(solution)/shard_map/all_to_all | solution.py:403
  46.3 23.1 %all-to-all-start.2 = ((f32[2,4,128,128]{2,1,0,3:T(4,128)}), f32[2,4,128,128]{2,1,0,3:T(4,128)S(1)}, u32[]{:S(2)}, u32[]{:S(2)}) async-start(f32[2,4,128,128]{2,1,0,3:T(4,128)} %copy.177), calls=%async_computation.2 | async-start | bytes 1048576 | tf_op jit(solution)/shard_map/all_to_all | solution.py:406
  72.2 20.6 %all-to-all-start.3 = ((f32[2,32,128,16]{2,3,0,1:T(8,128)}), f32[2,32,128,16]{2,3,0,1:T(8,128)S(1)}, u32[]{:S(2)}, u32[]{:S(2)}) async-start(f32[2,32,128,16]{2,3,0,1:T(8,128)} %copy.184), calls=%async_computation.3 | async-start | bytes 1048576 | tf_op jit(solution)/shard_map/all_to_all | solution.py:409
  93.1 1.0 copy-start
  100.0 13.9 %all-to-all-start.4 = ((f32[2,4,128,128]{3,1,0,2:T(4,128)}), f32[2,4,128,128]{3,1,0,2:T(4,128)S(1)}, u32[]{:S(2)}, u32[]{:S(2)}) async-start(f32[2,4,128,128]{3,1,0,2:T(4,128)} %copy.194), calls=%async_computation.4 | async-start | bytes 1048576 | tf_op jit(solution)/shard_map/all_to_all | solution.py:403
  130.1 19.3 %all-to-all-start.6 = ((f32[2,4,128,128]{2,1,0,3:T(4,128)}), f32[2,4,128,128]{2,1,0,3:T(4,128)S(1)}, u32[]{:S(2)}, u32[]{:S(2)}) async-start(f32[2,4,128,128]{2,1,0,3:T(4,128)} %copy.202), calls=%async_computation.6 | async-start | bytes 1048576 | tf_op jit(solution)/shard_map/all_to_all | solution.py:406
  152.2 17.4 %all-to-all-start.7 = ((f32[2,32,128,16]{2,3,0,1:T(8,128)}), f32[2,32,128,16]{2,3,0,1:T(8,128)S(1)}, u32[]{:S(2)}, u32[]{:S(2)}) async-start(f32[2,32,128,16]{2,3,0,1:T(8,128)} %copy.209), calls=%async_computation.7 | async-start | bytes 1048576 | tf_op jit(solution)/shard_map/all_to_all | solution.py:409
  176.1 15.2 %all-to-all-start.8 = ((f32[2,4,128,128]{3,1,0,2:T(4,128)}), f32[2,4,128,128]{3,1,0,2:T(4,128)S(1)}, u32[]{:S(2)}, u32[]{:S(2)}) async-start(f32[2,4,128,128]{3,1,0,2:T(4,128)} %copy.219), calls=%async_computation.8 | async-start | bytes 1048576 | tf_op jit(solution)/shard_map/all_to_all | solution.py:403
  207.4 17.2 %all-to-all-start.10 = ((f32[2,4,128,128]{2,1,0,3:T(4,128)}), f32[2,4,128,128]{2,1,0,3:T(4,128)S(1)}, u32[]{:S(2)}, u32[]{:S(2)}) async-start(f32[2,4,128,128]{2,1,0,3:T(4,128)} %copy.227), calls=%async_computation.10 | async-start | bytes 1048576 | tf_op jit(solution)/shard_map/all_to_all | solution.py:406
where the time goes:
time: 246 us; the launch traced here: 243 us
  waiting for transfers between devices  84.9 us (35%)
  blocking collectives  55.1 us (22%)
  starting transfers between devices  44.1 us (18%)
  matrix products  20.9 us (8%)
  between operations  17.6 us (7%)
  local copies, waits for them, and re-layouts  15.4 us (6%)
  other arithmetic  5.26 us (2%)
    all_to_all x3, waiting for transfers between devices, shards(): lax.all_to_all(values, 'qb', split_axis=3, concat_axis=1, tiled=True)  39.8 us
    all_to_all x3, blocking collectives, shards(): lax.all_to_all(moved, 'qa', split_axis=1, concat_axis=2, tiled=True)  39.6 us
    all_to_all x2, waiting for transfers between devices, shards(): lax.all_to_all(moved, 'qb', split_axis=1, concat_axis=3, tiled=True)  24.9 us
    all_to_all x3, starting transfers between devices, shards(): lax.all_to_all(values, 'qa', split_axis=2, concat_axis=1, tiled=True)  21.1 us
    dot_general x24, matrix products, times(): jnp.tensordot(values, table, axes=([dim], [0]), precision=lax.Precision.H...  20.9 us
    all_to_all x3, waiting for transfers between devices, shards(): lax.all_to_all(values, 'qa', split_axis=2, concat_axis=1, tiled=True)  20.2 us
    all_to_all x1, blocking collectives, shards(): lax.all_to_all(moved, 'qb', split_axis=1, concat_axis=3, tiled=True)  15.5 us
    all_to_all x3, starting transfers between devices, shards(): lax.all_to_all(values, 'qb', split_axis=3, concat_axis=1, tiled=True)  15.5 us
  transfers between devices with their start and end apart: 8, of which 8 were waited for; matrix products, arithmetic and copies ran while one was open for 0% of the time, Pallas kernels for 0%

commit v1 on v0

v1 whole, which is shorter than its diff:
```python
import functools

import jax
import jax.numpy as jnp
from jax import lax
from jax.experimental import pallas as pl
from jax.experimental.pallas import tpu as pltpu
from jax.sharding import PartitionSpec as P

LAYERS = 3
LANE, ROW, OUTER, MIDDLE = range(4)


def log2(count):
    return count.bit_length() - 1


def cos_sin(turn):
    half = 0.5 * turn
    y = half * half
    sine = -1 / 39916800
    for term in (1 / 362880, -1 / 5040, 1 / 120, -1 / 6, 1.0):
        sine = sine * y + term
    sine = sine * half
    cosine = 1 / 479001600
    for term in (-1 / 3628800, 1 / 40320, -1 / 720, 1 / 24, -0.5, 1.0):
        cosine = cosine * y + term
    return 1.0 - 2.0 * sine * sine, 2.0 * sine * cosine


def split(x):
    high = x.astype(jnp.bfloat16)
    return high, (x - high.astype(jnp.float32)).astype(jnp.bfloat16)


def dot(a, b, dims):
    return lax.dot_general(a, b, (dims, ((), ())), preferred_element_type=jnp.float32)


def right_weights(table):
    high, low = split(table)
    return jnp.concatenate(
        [jnp.concatenate([high, low], 1), jnp.concatenate([high, jnp.zeros_like(low)], 1)], 0)


def left_weights(table):
    high, low = split(table)
    return jnp.concatenate(
        [jnp.concatenate([high, high], 1), jnp.concatenate([low, jnp.zeros_like(low)], 1)], 0)


def times_right(x, weights):
    both = dot(jnp.concatenate(split(x), 1), weights, ((1,), (0,)))
    size = both.shape[1] // 2
    return both[:, :size] + both[:, size:]


def times_left(weights, x):
    both = dot(weights, jnp.concatenate(split(x), 0), ((1,), (0,)))
    size = both.shape[0] // 2
    return both[:size] + both[size:]


def times_left_turned(weights, x):
    both = dot(weights, jnp.concatenate(split(x), 1), ((1,), (1,)))
    size = both.shape[0] // 2
    return both[:size] + both[size:]


def turn_table(size, turns):
    out = lax.broadcasted_iota(jnp.int32, (8, size), 0)
    into = lax.broadcasted_iota(jnp.int32, (8, size), 1)
    table = None
    for i in range(3):
        c, s = turns[i]
        o, t = out >> i & 1, into >> i & 1
        factor = jnp.where(o == t, c, jnp.where(o > t, -s, s))
        table = factor if table is None else table * factor
    for i in range(3, log2(size)):
        c, s = turns[i]
        t = (into >> i & 1) == 0
        table = jnp.concatenate([_times(table, jnp.where(t, c, s)), _times(table, jnp.where(t, -s, c))], 0)
    return table


def _times(table, factor):
    rows = [table[i : i + 8] * factor for i in range(0, table.shape[0], 8)]
    return rows[0] if len(rows) == 1 else jnp.concatenate(rows, 0)


def mix_pair(u, v, turn):
    c, s = turn
    return c * u + s * v, c * v - s * u


def kernel(na, nb, wave_hbm, level_hbm, diag_hbm, turns_hbm, out, wave, level, diag, turns, in_sem,
           st, rt, s1, r1, s2, r2, s3, r3, cs, half, tables, send_sem, recv_sem):
    n = na * nb
    f32 = jnp.float32
    a = lax.axis_index("qa")
    b = lax.axis_index("qb")
    me = a * nb + b

    def peer_of(k):
        pa = lax.rem(a + lax.div(k, nb), na)
        pb = lax.rem(b + lax.rem(k, nb), nb)
        return pa * nb + pb, {"qa": pa, "qb": pb}

    fetched = [
        pltpu.make_async_copy(src, dst, in_sem.at[i])
        for i, (src, dst) in enumerate(
            ((turns_hbm, turns), (level_hbm, level), (diag_hbm, diag), (wave_hbm, wave)))
    ]
    for copy in fetched:
        copy.start()

    barrier = pltpu.get_barrier_semaphore()

    def greet(k, carry):
        pl.semaphore_signal(barrier, inc=1, device_id=peer_of(k)[1], device_id_type=pl.DeviceIdType.MESH)
        return carry

    lax.fori_loop(1, n, greet, 0)

    def tile(ref, i, part):
        first, count = part
        return ref.at[pl.ds(pl.multiple_of(i * 8, 8) + first, count)]

    def send(src, dst, which, part):
        def step(k, carry):
            peer, to = peer_of(k)
            pltpu.make_async_remote_copy(
                src_ref=tile(src, peer, part), dst_ref=tile(dst, me, part), send_sem=send_sem.at[which],
                recv_sem=recv_sem.at[which], device_id=to, device_id_type=pl.DeviceIdType.MESH).start()
            return carry

        lax.fori_loop(1, n, step, 0)
        first, count = part
        dst[pl.ds(pl.multiple_of(me * 8, 8), 8), :] = src[pl.ds(pl.multiple_of(me * 8, 8), 8), :]

    def total(ref, sem, part):
        whole = ref.at[pl.ds(0, (n - 1) * part[1])]
        return pltpu.make_async_copy(whole, whole, sem)

    def arrive(dst, which, part):
        total(dst, recv_sem.at[which], part).wait()

    def sent(src, which, part):
        total(src, send_sem.at[which], part).wait()

    FULL, LOW, HIGH = (0, 8), (0, 4), (4, 4)

    def plane(j):
        return pl.ds(j, n, stride=8)

    fetched[0].wait()
    angle = [[cos_sin(jnp.full((1, n), turns[layer, g], f32)) for g in range(4)] for layer in range(LAYERS)]
    bits = log2(n)

    def lane_turns(layer):
        return [angle[layer][LANE]] * bits

    def row_turns(layer):
        return [angle[layer][ROW]] * bits

    def device_turns(layer):
        return [angle[layer][MIDDLE]] * log2(nb) + [angle[layer][OUTER]] * log2(na)

    def back(turn_list):
        return [(c, -s) for c, s in turn_list]

    tables[0] = right_weights(turn_table(n, back(lane_turns(0))))
    tables[1] = left_weights(turn_table(n, row_turns(0)))

    pop = jnp.zeros((8, n), jnp.int32)
    row8 = lax.broadcasted_iota(jnp.int32, (8, n), 0)
    lane8 = lax.broadcasted_iota(jnp.int32, (8, n), 1)
    for i in range(3):
        pop = pop + (row8 >> i & 1)
    for i in range(bits):
        pop = pop + (lane8 >> i & 1) + lax.rem(lax.div(me, 1 << i), 2)
    pop = pop & 3
    fr = jnp.where(pop == 0, 1.0, jnp.where(pop == 2, -1.0, 0.0))
    fi = jnp.where(pop == 1, -1.0, jnp.where(pop == 3, 1.0, 0.0))
    quarter = [(fr, fi), (fi, -fr), (-fr, -fi), (-fi, fr)]

    def power(block):
        picks = [quarter[(v.bit_count() + block.bit_count()) % 4] for v in range(n // 8)]
        return [jnp.concatenate([p[i] for p in picks], 0) if len(picks) > 1 else picks[0][i] for i in range(2)]

    fetched[1].wait()
    for g in range(4):
        st[plane(g), :] = level[g]
    pl.semaphore_wait(barrier, n - 1)
    send(st, rt, 0, LOW)

    fetched[2].wait()
    fetched[3].wait()
    planes = [[], []]
    for g in range(4):
        c, s = cos_sin(diag[0:1, :] * level[g])
        re, im = wave[0, g], wave[1, g]
        re, im = re * c + im * s, im * c - re * s
        pr, pi = power(g)
        planes[0].append(re * pr - im * pi)
        planes[1].append(im * pr + re * pi)

    def mix_blocks(xs, turn):
        xs[0], xs[2] = mix_pair(xs[0], xs[2], turn)
        xs[1], xs[3] = mix_pair(xs[1], xs[3], turn)
        xs[0], xs[1] = mix_pair(xs[0], xs[1], turn)
        xs[2], xs[3] = mix_pair(xs[2], xs[3], turn)
        return xs

    def columns(x):
        return [x[:, i : i + n] for i in range(0, x.shape[1], n)]

    for p in range(2):
        x = times_right(jnp.concatenate(planes[p], 0), tables[0])
        x = jnp.concatenate([x[g * n : (g + 1) * n] for g in range(4)], 1)
        x = times_left(tables[1], x)
        for g, x in enumerate(mix_blocks(columns(x), angle[0][OUTER])):
            s1[plane(p * 4 + g), :] = x
    send(s1, r1, 1, FULL)

    for g in range(4):
        st[plane(4 + g), :] = level[g].T
    send(st, rt, 2, HIGH)

    tables[2] = left_weights(turn_table(n, device_turns(0)))
    tables[3] = left_weights(turn_table(n, device_turns(1)))
    tables[4] = left_weights(turn_table(n, lane_turns(1)))

    arrive(rt, 0, LOW)
    for g in range(4):
        c, s = cos_sin(diag[1:2, :] * rt[plane(g), :])
        cs[0, g] = c
        cs[1, g] = s

    arrive(r1, 1, FULL)
    for p in range(2):
        x = jnp.concatenate([r1[plane(p * 4 + g), :] for g in range(4)], 1)
        x = times_left(tables[2], x)
        for g, x in enumerate(columns(x)):
            half[p, g] = x
    turned = [[], []]
    for g in range(4):
        re, im = half[0, g], half[1, g]
        c, s = cs[0, g], cs[1, g]
        turned[0].append(re * c + im * s)
        turned[1].append(im * c - re * s)
    for p in range(2):
        x = times_left(tables[3], jnp.concatenate(turned[p], 1))
        x = times_left_turned(tables[4], jnp.concatenate(columns(x), 0))
        for g, x in enumerate(mix_blocks(columns(x), angle[1][OUTER])):
            s2[plane((g % 2) * 4 + p * 2 + g // 2), :] = x
    send(s2, r2, 3, LOW)
    send(s2, r2, 4, HIGH)

    tables[5] = left_weights(turn_table(n, row_turns(1)))
    tables[6] = left_weights(turn_table(n, row_turns(2)))
    tables[7] = left_weights(turn_table(n, device_turns(2)))
    tables[8] = left_weights(turn_table(n, lane_turns(2)))

    lane1 = lax.broadcasted_iota(jnp.int32, (1, n), 1)
    own = jnp.sum(jnp.where(lane1 == me, diag[2:3, :], 0.0), axis=1, keepdims=True)
    arrive(rt, 2, HIGH)
    for g in range(4):
        c, s = cos_sin(own * rt[plane(4 + g), :].T)
        cs[0, g] = c
        cs[1, g] = s

    for q, part in enumerate((LOW, HIGH)):
        arrive(r2, 3 + q, part)
        pair = []
        for p in range(2):
            x = jnp.concatenate([r2[plane(q * 4 + p * 2 + g), :] for g in range(2)], 1)
            pair.append(columns(times_left(tables[5], x)))
        turned = [[], []]
        for g in range(2):
            re, im = pair[0][g], pair[1][g]
            c, s = cs[0, g * 2 + q], cs[1, g * 2 + q]
            turned[0].append(re * c + im * s)
            turned[1].append(im * c - re * s)
        for p in range(2):
            x = times_left(tables[6], jnp.concatenate(turned[p], 1))
            x = times_left_turned(tables[7], jnp.concatenate(columns(x), 0))
            for g, x in enumerate(mix_pair(*columns(x), angle[2][OUTER])):
                s3[plane(q * 4 + p * 2 + g), :] = x
        send(s3, r3, 5 + q, part)

    for q, part in enumerate((LOW, HIGH)):
        arrive(r3, 5 + q, part)
        for p in range(2):
            x = jnp.concatenate([r3[plane(q * 4 + p * 2 + g), :] for g in range(2)], 1)
            for g, x in enumerate(columns(times_left(tables[8], x))):
                half[p, g * 2 + q] = x.T
    for h in range(2):
        pairs = [mix_pair(half[p, h * 2], half[p, h * 2 + 1], angle[2][OUTER]) for p in range(2)]
        for q in range(2):
            re, im = pairs[0][q], pairs[1][q]
            pr, pi = power(h * 2 + q)
            out[0, h * 2 + q] = re * pr + im * pi
            out[1, h * 2 + q] = im * pr - re * pi

    sent(st, 0, LOW)
    sent(s1, 1, FULL)
    sent(st, 2, HIGH)
    for q, part in enumerate((LOW, HIGH)):
        sent(s2, 3 + q, part)
        sent(s3, 5 + q, part)


def fused(wave_parts, level_table, diagonal_angles, turn_angles, na, nb):
    n = na * nb
    f32 = jnp.float32
    V = pltpu.VMEM
    tiles = V((n * 8, n), f32)
    return pl.pallas_call(
        functools.partial(kernel, na, nb),
        out_shape=jax.ShapeDtypeStruct(wave_parts.shape, f32),
        in_specs=[pl.BlockSpec(memory_space=pltpu.HBM)] * 4,
        out_specs=pl.BlockSpec(memory_space=pltpu.VMEM),
        scratch_shapes=[
            V(wave_parts.shape, f32), V(level_table.shape, f32), V(diagonal_angles.shape, f32),
            pltpu.SMEM(turn_angles.shape, f32), pltpu.SemaphoreType.DMA((4,)),
            tiles, tiles, tiles, tiles, tiles, tiles, tiles, tiles,
            V((2,) + level_table.shape, f32), V(wave_parts.shape, f32),
            V((9, 2 * n, 2 * n), jnp.bfloat16),
            pltpu.SemaphoreType.DMA((7,)), pltpu.SemaphoreType.DMA((7,)),
        ],
        compiler_params=pltpu.CompilerParams(
            collective_id=0, has_side_effects=True, vmem_limit_bytes=32 * 1024 * 1024),
    )(wave_parts, level_table, diagonal_angles, turn_angles)


def solution(mesh):
    na, nb = mesh.shape["qa"], mesh.shape["qb"]

    def each(wave_parts, level_table, diagonal_angles, turn_angles):
        return fused(wave_parts, level_table, diagonal_angles, turn_angles, na, nb)

    placed = (
        P("trial", ("qa", "qb"), None, None),
        P(("trial", "qa", "qb"), None, None),
        P("trial", None),
        P("trial", None),
    )
    return jax.shard_map(
        each,
        mesh=mesh,
        in_specs=placed,
        out_specs=P("trial", ("qa", "qb"), None, None),
        check_vma=False,
    )
```

time: 246 us -> 67.1 us (0.27)
  waiting for transfers between devices: 84.9 us -> 0 us
  Pallas kernels: 0 us -> 62.5 us
  blocking collectives: 55.1 us -> 0 us
  starting transfers between devices: 44.1 us -> 0 us
  matrix products: 20.9 us -> 0 us
  between operations: 17.6 us -> 0.01 us
  local copies, waits for them, and re-layouts: 15.4 us -> 4.15 us
  other arithmetic: 5.26 us -> 0 us
    all_to_all x8 -> x0, waiting for transfers between devices: 84.9 us -> none  [the longest x3 39.8 us: shards(): lax.all_to_all(values, 'qb', split_axis=3, concat_axis=1, tiled=True)]
    pallas_call x0 -> x1, Pallas kernels: none -> 62.5 us  [fused(): pl.pallas_call(functools.partial(kernel, na, nb), out_shape=jax.ShapeDtyp...]
    all_to_all x4 -> x0, blocking collectives: 55.1 us -> none  [the longest x3 39.6 us: shards(): lax.all_to_all(moved, 'qa', split_axis=1, concat_axis=2, tiled=True)]
    all_to_all x8 -> x0, starting transfers between devices: 44.1 us -> none  [the longest x3 21.1 us: shards(): lax.all_to_all(values, 'qa', split_axis=2, concat_axis=1, tiled=True)]
    dot_general x24 -> x0, matrix products: 20.9 us -> none  [times(): jnp.tensordot(values, table, axes=([dim], [0]), precision=lax.Precision.H...]
    another operation x9 -> x0, local copies, waits for them, and re-layouts: 5.69 us -> none  [mix_dim(): return jnp.stack([by_real[0] - by_imag[1], by_real[1] + by_imag[0]])]
    all_to_all x16 -> x0, local copies, waits for them, and re-layouts: 5.52 us -> none  [the longest x6 3.09 us: shards(): lax.all_to_all(moved, 'qa', split_axis=1, concat_axis=2, tiled=True)]
    another operation x12 -> x0, other arithmetic: 4.42 us -> none  [the longest x3 4.08 us: phase_step(): jnp.stack([values[0] * jnp.cos(turn) + values[1] * jnp.sin(turn), values[...]
  transfers between devices with their start and end apart: 8 -> 0, of which waited for: 8 -> 0; matrix products, arithmetic and copies ran while one was open for 0% -> 0% of each run, Pallas kernels for 0% -> 0%
where the time goes in v1:
time: 67.1 us; the launch traced here: 66.7 us
  Pallas kernels  62.5 us (93%)
  local copies, waits for them, and re-layouts  4.15 us (6%)
    pallas_call x1, Pallas kernels, fused(): pl.pallas_call(functools.partial(kernel, na, nb), out_shape=jax.ShapeDtyp...  62.5 us
    unnamed x9, local copies, waits for them, and re-layouts  4.15 us

profile of v1, /device:TPU:8, one launch (start us, length us, event | category | flops | bytes accessed | tf_op | source)
XLA Modules:
  0.0 66.7 jit_solution(6359478304916248667)
XLA Ops:
  0.0 0.0 copy-start
  0.0 1.0 %copy-done = f32[2,4,128,128]{3,2,1,0:T(8,128)S(1)} copy-done((f32[2,4,128,128]{3,2,1,0:T(8,128)S(1)}, f32[2,4,128,128]{3,2,1,0:T(8,128)}, u32[]{:S(2)}) %copy-start) | copy-done | bytes 524312
  1.0 0.0 copy-start.1
  1.0 0.9 %copy-done.1 = f32[4,128,128]{2,1,0:T(8,128)S(1)} copy-done((f32[4,128,128]{2,1,0:T(8,128)S(1)}, f32[4,128,128]{2,1,0:T(8,128)}, u32[]{:S(2)}) %copy-start.1) | copy-done | bytes 262168
  2.0 0.0 copy-start.2
  2.0 0.7 %copy-done.2 = f32[3,128]{1,0:T(4,128)S(1)} copy-done((f32[3,128]{1,0:T(4,128)S(1)}, f32[3,128]{1,0:T(4,128)}, u32[]{:S(2)}) %copy-start.2) | copy-done | bytes 1560
  2.7 0.0 copy-start.3
  2.7 0.7 %copy-done.3 = f32[3,4]{1,0:T(4,128)S(1)} copy-done((f32[3,4]{1,0:T(4,128)S(1)}, f32[3,4]{1,0:T(4,128)}, u32[]{:S(2)}) %copy-start.3) | copy-done | bytes 72
  3.4 62.5 %shard_map.46 = f32[2,4,128,128]{3,2,1,0:T(8,128)S(1)} custom-call(f32[2,4,128,128]{3,2,1,0:T(8,128)S(1)} %copy-done, f32[4,128,128]{2,1,0:T(8,128)S(1)} %copy-done.1, f32[3,128]{1,0:T(4,128)S(1)} %copy-done.2, f32[3,4]{1,0:T(4,128)S(1)} %copy-done.3), custom_call_target="tpu_custom_call" | custom-call | tf_op jit(solution)/shard_map/pallas_call | solution.py:319
  65.9 0.8 %copy.6 = f32[2,4,128,128]{3,2,1,0:T(8,128)} copy(f32[2,4,128,128]{3,2,1,0:T(8,128)S(1)} %shard_map.46) | data formatting | bytes 1048576
Async XLA Ops:
  0.0 1.0 %copy-start = (f32[2,4,128,128]{3,2,1,0:T(8,128)S(1)}, f32[2,4,128,128]{3,2,1,0:T(8,128)}, u32[]{:S(2)}) copy-start(f32[2,4,128,128]{3,2,1,0:T(8,128)} %wave_hbm.1) | copy-start | bytes 1572868
  1.0 0.9 %copy-start.1 = (f32[4,128,128]{2,1,0:T(8,128)S(1)}, f32[4,128,128]{2,1,0:T(8,128)}, u32[]{:S(2)}) copy-start(f32[4,128,128]{2,1,0:T(8,128)} %level_hbm.1) | copy-start | bytes 786436
  2.0 0.7 %copy-start.2 = (f32[3,128]{1,0:T(4,128)S(1)}, f32[3,128]{1,0:T(4,128)}, u32[]{:S(2)}) copy-start(f32[3,128]{1,0:T(4,128)} %diag_hbm.1) | copy-start | bytes 4612
  2.7 0.7 %copy-start.3 = (f32[3,4]{1,0:T(4,128)S(1)}, f32[3,4]{1,0:T(4,128)}, u32[]{:S(2)}) copy-start(f32[3,4]{1,0:T(4,128)} %turns_hbm.1) | copy-start | bytes 148

commit v2 on v1

--- a/solution.py
+++ b/solution.py
@@ -101,10 +101,18 @@
     b = lax.axis_index("qb")
     me = a * nb + b
 
-    def peer_of(k):
-        pa = lax.rem(a + lax.div(k, nb), na)
-        pb = lax.rem(b + lax.rem(k, nb), nb)
-        return pa * nb + pb, {"qa": pa, "qb": pb}
+    places = [lax.rem(b + j, nb) for j in range(nb)]
+    away = sorted(range(1, nb), key=lambda j: -min(j, nb - j))
+
+    def each_peer(visit):
+        def step(i, carry, shifts):
+            pa = lax.rem(a + i, na)
+            for j in shifts:
+                visit(pa * nb + places[j], {"qa": pa, "qb": places[j]})
+            return carry
+
+        step(0, 0, away)
+        lax.fori_loop(1, na, functools.partial(step, shifts=[0] + away), 0)
 
     fetched = [
         pltpu.make_async_copy(src, dst, in_sem.at[i])
@@ -116,27 +124,24 @@
 
     barrier = pltpu.get_barrier_semaphore()
 
-    def greet(k, carry):
-        pl.semaphore_signal(barrier, inc=1, device_id=peer_of(k)[1], device_id_type=pl.DeviceIdType.MESH)
-        return carry
-
-    lax.fori_loop(1, n, greet, 0)
+    def greet(peer, to):
+        pl.semaphore_signal(barrier, inc=1, device_id=to, device_id_type=pl.DeviceIdType.MESH)
+
+    each_peer(greet)
 
     def tile(ref, i, part):
         first, count = part
         return ref.at[pl.ds(pl.multiple_of(i * 8, 8) + first, count)]
 
     def send(src, dst, which, part):
-        def step(k, carry):
-            peer, to = peer_of(k)
+        def visit(peer, to):
             pltpu.make_async_remote_copy(
                 src_ref=tile(src, peer, part), dst_ref=tile(dst, me, part), send_sem=send_sem.at[which],
                 recv_sem=recv_sem.at[which], device_id=to, device_id_type=pl.DeviceIdType.MESH).start()
-            return carry
-
-        lax.fori_loop(1, n, step, 0)
-        first, count = part
-        dst[pl.ds(pl.multiple_of(me * 8, 8), 8), :] = src[pl.ds(pl.multiple_of(me * 8, 8), 8), :]
+
+        each_peer(visit)
+        own = pl.ds(pl.multiple_of(me * 8, 8), 8)
+        dst[own, :] = src[own, :]
 
     def total(ref, sem, part):
         whole = ref.at[pl.ds(0, (n - 1) * part[1])]
@@ -191,9 +196,6 @@
     fetched[1].wait()
     for g in range(4):
         st[plane(g), :] = level[g]
-    pl.semaphore_wait(barrier, n - 1)
-    send(st, rt, 0, LOW)
-
     fetched[2].wait()
     fetched[3].wait()
     planes = [[], []]
@@ -221,6 +223,8 @@
         x = times_left(tables[1], x)
         for g, x in enumerate(mix_blocks(columns(x), angle[0][OUTER])):
             s1[plane(p * 4 + g), :] = x
+    pl.semaphore_wait(barrier, n - 1)
+    send(st, rt, 0, LOW)
     send(s1, r1, 1, FULL)
 
     for g in range(4):
@@ -316,6 +320,10 @@
     f32 = jnp.float32
     V = pltpu.VMEM
     tiles = V((n * 8, n), f32)
+    inputs = [
+        pltpu.with_memory_space_constraint(x, pltpu.HBM)
+        for x in (wave_parts, level_table, diagonal_angles, turn_angles)
+    ]
     return pl.pallas_call(
         functools.partial(kernel, na, nb),
         out_shape=jax.ShapeDtypeStruct(wave_parts.shape, f32),
@@ -331,7 +339,7 @@
         ],
         compiler_params=pltpu.CompilerParams(
             collective_id=0, has_side_effects=True, vmem_limit_bytes=32 * 1024 * 1024),
-    )(wave_parts, level_table, diagonal_angles, turn_angles)
+    )(*inputs)
 
 
 def solution(mesh):

time: 67.1 us -> 62.1 us (0.925)
  local copies, waits for them, and re-layouts: 4.15 us -> 0.8 us
  Pallas kernels: 62.5 us -> 61.2 us
    unnamed x9 -> x1, local copies, waits for them, and re-layouts: 4.15 us -> 0.8 us
    pallas_call x1, Pallas kernels: 62.5 us -> 61.2 us  [fused(): pl.pallas_call(functools.partial(kernel, na, nb), out_shape=jax.ShapeDtyp...]
where the time goes in v2:
time: 62.1 us; the launch traced here: 62 us
  Pallas kernels  61.2 us (99%)
  local copies, waits for them, and re-layouts  0.8 us (1%)
    pallas_call x1, Pallas kernels, fused(): pl.pallas_call(functools.partial(kernel, na, nb), out_shape=jax.ShapeDtyp...  61.2 us

profile of v2, /device:TPU:8, one launch (start us, length us, event | category | flops | bytes accessed | tf_op | source)
XLA Modules:
  0.0 62.0 jit_solution(2665282333242089428)
XLA Ops:
  0.0 61.2 %shard_map.46 = f32[2,4,128,128]{3,2,1,0:T(8,128)S(1)} custom-call(f32[2,4,128,128]{3,2,1,0:T(8,128)} %wave_hbm.1, f32[4,128,128]{2,1,0:T(8,128)} %level_hbm.1, f32[3,128]{1,0:T(4,128)} %diag_hbm.1, f32[3,4]{1,0:T(4,128)} %turns_hbm.1), custom_call_target="tpu_custom_call" | custom-call | tf_op jit(solution)/shard_map/pallas_call | solution.py:327
  61.2 0.8 %copy.6 = f32[2,4,128,128]{3,2,1,0:T(8,128)} copy(f32[2,4,128,128]{3,2,1,0:T(8,128)S(1)} %shard_map.46) | data formatting | bytes 1048576

commit v3 on v2

--- a/solution.py
+++ b/solution.py
@@ -114,6 +114,18 @@
         step(0, 0, away)
         lax.fori_loop(1, na, functools.partial(step, shifts=[0] + away), 0)
 
+    def each_peer_by_plane(visit):
+        def step(i, carry, planes):
+            pa = lax.rem(a + i, na)
+            for pb in planes:
+                visit(pa * nb + pb, {"qa": pa, "qb": pb})
+            return carry
+
+        for j in away:
+            visit(a * nb + places[j], {"qa": a, "qb": places[j]})
+        for planes in (range(nb // 2), range(nb // 2, nb)):
+            lax.fori_loop(1, na, functools.partial(step, planes=planes), 0)
+
     fetched = [
         pltpu.make_async_copy(src, dst, in_sem.at[i])
         for i, (src, dst) in enumerate(
@@ -131,16 +143,18 @@
 
     def tile(ref, i, part):
         first, count = part
-        return ref.at[pl.ds(pl.multiple_of(i * 8, 8) + first, count)]
-
-    def send(src, dst, which, part):
+        step = ref.shape[0] // n
+        return ref.at[pl.ds(pl.multiple_of(i * step, 8) + first, count)]
+
+    def send(src, dst, which, part, each=each_peer):
         def visit(peer, to):
             pltpu.make_async_remote_copy(
                 src_ref=tile(src, peer, part), dst_ref=tile(dst, me, part), send_sem=send_sem.at[which],
                 recv_sem=recv_sem.at[which], device_id=to, device_id_type=pl.DeviceIdType.MESH).start()
 
-        each_peer(visit)
-        own = pl.ds(pl.multiple_of(me * 8, 8), 8)
+        each(visit)
+        step = src.shape[0] // n
+        own = pl.ds(pl.multiple_of(me * step, 8), step)
         dst[own, :] = src[own, :]
 
     def total(ref, sem, part):
@@ -153,10 +167,10 @@
     def sent(src, which, part):
         total(src, send_sem.at[which], part).wait()
 
-    FULL, LOW, HIGH = (0, 8), (0, 4), (4, 4)
-
-    def plane(j):
-        return pl.ds(j, n, stride=8)
+    WITH_LEVELS, LOW, HIGH = (0, 12), (0, 4), (4, 4)
+
+    def plane(j, step=8):
+        return pl.ds(j, n, stride=step)
 
     fetched[0].wait()
     angle = [[cos_sin(jnp.full((1, n), turns[layer, g], f32)) for g in range(4)] for layer in range(LAYERS)]
@@ -195,7 +209,8 @@
 
     fetched[1].wait()
     for g in range(4):
-        st[plane(g), :] = level[g]
+        s1[plane(8 + g, 16), :] = level[g]
+        st[plane(g), :] = level[g].T
     fetched[2].wait()
     fetched[3].wait()
     planes = [[], []]
@@ -222,35 +237,25 @@
         x = jnp.concatenate([x[g * n : (g + 1) * n] for g in range(4)], 1)
         x = times_left(tables[1], x)
         for g, x in enumerate(mix_blocks(columns(x), angle[0][OUTER])):
-            s1[plane(p * 4 + g), :] = x
+            s1[plane(p * 4 + g, 16), :] = x
     pl.semaphore_wait(barrier, n - 1)
-    send(st, rt, 0, LOW)
-    send(s1, r1, 1, FULL)
-
-    for g in range(4):
-        st[plane(4 + g), :] = level[g].T
-    send(st, rt, 2, HIGH)
+    send(s1, r1, 0, WITH_LEVELS)
+    send(st, rt, 1, LOW)
 
     tables[2] = left_weights(turn_table(n, device_turns(0)))
     tables[3] = left_weights(turn_table(n, device_turns(1)))
     tables[4] = left_weights(turn_table(n, lane_turns(1)))
 
-    arrive(rt, 0, LOW)
-    for g in range(4):
-        c, s = cos_sin(diag[1:2, :] * rt[plane(g), :])
-        cs[0, g] = c
-        cs[1, g] = s
-
-    arrive(r1, 1, FULL)
+    arrive(r1, 0, WITH_LEVELS)
     for p in range(2):
-        x = jnp.concatenate([r1[plane(p * 4 + g), :] for g in range(4)], 1)
+        x = jnp.concatenate([r1[plane(p * 4 + g, 16), :] for g in range(4)], 1)
         x = times_left(tables[2], x)
         for g, x in enumerate(columns(x)):
             half[p, g] = x
     turned = [[], []]
     for g in range(4):
         re, im = half[0, g], half[1, g]
-        c, s = cs[0, g], cs[1, g]
+        c, s = cos_sin(diag[1:2, :] * r1[plane(8 + g, 16), :])
         turned[0].append(re * c + im * s)
         turned[1].append(im * c - re * s)
     for p in range(2):
@@ -258,8 +263,8 @@
         x = times_left_turned(tables[4], jnp.concatenate(columns(x), 0))
         for g, x in enumerate(mix_blocks(columns(x), angle[1][OUTER])):
             s2[plane((g % 2) * 4 + p * 2 + g // 2), :] = x
-    send(s2, r2, 3, LOW)
-    send(s2, r2, 4, HIGH)
+    send(s2, r2, 2, LOW)
+    send(s2, r2, 3, HIGH)
 
     tables[5] = left_weights(turn_table(n, row_turns(1)))
     tables[6] = left_weights(turn_table(n, row_turns(2)))
@@ -268,14 +273,14 @@
 
     lane1 = lax.broadcasted_iota(jnp.int32, (1, n), 1)
     own = jnp.sum(jnp.where(lane1 == me, diag[2:3, :], 0.0), axis=1, keepdims=True)
-    arrive(rt, 2, HIGH)
+    arrive(rt, 1, LOW)
     for g in range(4):
-        c, s = cos_sin(own * rt[plane(4 + g), :].T)
+        c, s = cos_sin(own * rt[plane(g), :].T)
         cs[0, g] = c
         cs[1, g] = s
 
     for q, part in enumerate((LOW, HIGH)):
-        arrive(r2, 3 + q, part)
+        arrive(r2, 2 + q, part)
         pair = []
         for p in range(2):
             x = jnp.concatenate([r2[plane(q * 4 + p * 2 + g), :] for g in range(2)], 1)
@@ -291,10 +296,10 @@
             x = times_left_turned(tables[7], jnp.concatenate(columns(x), 0))
             for g, x in enumerate(mix_pair(*columns(x), angle[2][OUTER])):
                 s3[plane(q * 4 + p * 2 + g), :] = x
-        send(s3, r3, 5 + q, part)
+        send(s3, r3, 4 + q, part, (each_peer, each_peer_by_plane)[q])
 
     for q, part in enumerate((LOW, HIGH)):
-        arrive(r3, 5 + q, part)
+        arrive(r3, 4 + q, part)
         for p in range(2):
             x = jnp.concatenate([r3[plane(q * 4 + p * 2 + g), :] for g in range(2)], 1)
             for g, x in enumerate(columns(times_left(tables[8], x))):
@@ -307,19 +312,18 @@
             out[0, h * 2 + q] = re * pr + im * pi
             out[1, h * 2 + q] = im * pr - re * pi
 
-    sent(st, 0, LOW)
-    sent(s1, 1, FULL)
-    sent(st, 2, HIGH)
+    sent(s1, 0, WITH_LEVELS)
+    sent(st, 1, LOW)
     for q, part in enumerate((LOW, HIGH)):
-        sent(s2, 3 + q, part)
-        sent(s3, 5 + q, part)
+        sent(s2, 2 + q, part)
+        sent(s3, 4 + q, part)
 
 
 def fused(wave_parts, level_table, diagonal_angles, turn_angles, na, nb):
     n = na * nb
     f32 = jnp.float32
     V = pltpu.VMEM
-    tiles = V((n * 8, n), f32)
+    tiles, tall = V((n * 8, n), f32), V((n * 16, n), f32)
     inputs = [
         pltpu.with_memory_space_constraint(x, pltpu.HBM)
         for x in (wave_parts, level_table, diagonal_angles, turn_angles)
@@ -332,10 +336,10 @@
         scratch_shapes=[
             V(wave_parts.shape, f32), V(level_table.shape, f32), V(diagonal_angles.shape, f32),
             pltpu.SMEM(turn_angles.shape, f32), pltpu.SemaphoreType.DMA((4,)),
-            tiles, tiles, tiles, tiles, tiles, tiles, tiles, tiles,
+            tiles, tiles, tall, tall, tiles, tiles, tiles, tiles,
             V((2,) + level_table.shape, f32), V(wave_parts.shape, f32),
             V((9, 2 * n, 2 * n), jnp.bfloat16),
-            pltpu.SemaphoreType.DMA((7,)), pltpu.SemaphoreType.DMA((7,)),
+            pltpu.SemaphoreType.DMA((6,)), pltpu.SemaphoreType.DMA((6,)),
         ],
         compiler_params=pltpu.CompilerParams(
             collective_id=0, has_side_effects=True, vmem_limit_bytes=32 * 1024 * 1024),

time: 62.1 us -> 61.3 us (0.987)
  Pallas kernels: 61.2 us -> 60.4 us
    pallas_call x1, Pallas kernels: 61.2 us -> 60.4 us  [fused(): pl.pallas_call(functools.partial(kernel, na, nb), out_shape=jax.ShapeDtyp...]
where the time goes in v3:
time: 61.3 us; the launch traced here: 61.2 us
  Pallas kernels  60.4 us (99%)
  local copies, waits for them, and re-layouts  0.8 us (1%)
    pallas_call x1, Pallas kernels, fused(): pl.pallas_call(functools.partial(kernel, na, nb), out_shape=jax.ShapeDtyp...  60.4 us

profile of v3, /device:TPU:8, one launch (start us, length us, event | category | flops | bytes accessed | tf_op | source)
XLA Modules:
  0.0 61.2 jit_solution(375033809325048337)
XLA Ops:
  0.0 60.4 %shard_map.46 = f32[2,4,128,128]{3,2,1,0:T(8,128)S(1)} custom-call(f32[2,4,128,128]{3,2,1,0:T(8,128)} %wave_hbm.1, f32[4,128,128]{2,1,0:T(8,128)} %level_hbm.1, f32[3,128]{1,0:T(4,128)} %diag_hbm.1, f32[3,4]{1,0:T(4,128)} %turns_hbm.1), custom_call_target="tpu_custom_call" | custom-call | tf_op jit(solution)/shard_map/pallas_call | solution.py:331
  60.4 0.8 %copy.6 = f32[2,4,128,128]{3,2,1,0:T(8,128)} copy(f32[2,4,128,128]{3,2,1,0:T(8,128)S(1)} %shard_map.46) | data formatting | bytes 1048576

commit v4 on v3

--- a/solution.py
+++ b/solution.py
@@ -99,31 +99,39 @@
     f32 = jnp.float32
     a = lax.axis_index("qa")
     b = lax.axis_index("qb")
+    trial = lax.axis_index("trial")
     me = a * nb + b
 
     places = [lax.rem(b + j, nb) for j in range(nb)]
     away = sorted(range(1, nb), key=lambda j: -min(j, nb - j))
 
-    def each_peer(visit):
+    def each_peer(visit, farthest=False):
         def step(i, carry, shifts):
             pa = lax.rem(a + i, na)
             for j in shifts:
                 visit(pa * nb + places[j], {"qa": pa, "qb": places[j]})
             return carry
 
+        row = functools.partial(step, shifts=[0] + away)
+        if farthest:
+            lax.fori_loop(na // 2, na, row, 0)
         step(0, 0, away)
-        lax.fori_loop(1, na, functools.partial(step, shifts=[0] + away), 0)
+        lax.fori_loop(1, na // 2 if farthest else na, row, 0)
 
     def each_peer_by_plane(visit):
+        start = trial * (nb // 2)
+        quarter = max(1, nb // 4)
+
         def step(i, carry, planes):
             pa = lax.rem(a + i, na)
-            for pb in planes:
+            for j in planes:
+                pb = lax.rem(start + j, nb)
                 visit(pa * nb + pb, {"qa": pa, "qb": pb})
             return carry
 
         for j in away:
             visit(a * nb + places[j], {"qa": a, "qb": places[j]})
-        for planes in (range(nb // 2), range(nb // 2, nb)):
+        for planes in (range(quarter), range(quarter, nb // 2), range(nb // 2, nb)):
             lax.fori_loop(1, na, functools.partial(step, planes=planes), 0)
 
     fetched = [
@@ -139,7 +147,7 @@
     def greet(peer, to):
         pl.semaphore_signal(barrier, inc=1, device_id=to, device_id_type=pl.DeviceIdType.MESH)
 
-    each_peer(greet)
+    each_peer(greet, farthest=True)
 
     def tile(ref, i, part):
         first, count = part

time: 61.3 us -> 63.3 us (1.033)
  Pallas kernels: 60.4 us -> 62.1 us
    pallas_call x1, Pallas kernels: 60.4 us -> 62.1 us  [fused(): pl.pallas_call(functools.partial(kernel, na, nb), out_shape=jax.ShapeDtyp...]
where the time goes in v4:
time: 63.3 us; the launch traced here: 62.9 us
  Pallas kernels  62.1 us (98%)
  local copies, waits for them, and re-layouts  0.8 us (1%)
    pallas_call x1, Pallas kernels, fused(): pl.pallas_call(functools.partial(kernel, na, nb), out_shape=jax.ShapeDtyp...  62.1 us

profile of v4, /device:TPU:8, one launch (start us, length us, event | category | flops | bytes accessed | tf_op | source)
XLA Modules:
  0.0 62.9 jit_solution(2204924069395275910)
XLA Ops:
  0.0 62.1 %shard_map.46 = f32[2,4,128,128]{3,2,1,0:T(8,128)S(1)} custom-call(f32[2,4,128,128]{3,2,1,0:T(8,128)} %wave_hbm.1, f32[4,128,128]{2,1,0:T(8,128)} %level_hbm.1, f32[3,128]{1,0:T(4,128)} %diag_hbm.1, f32[3,4]{1,0:T(4,128)} %turns_hbm.1), custom_call_target="tpu_custom_call" | custom-call | tf_op jit(solution)/shard_map/pallas_call | solution.py:339
  62.1 0.8 %copy.6 = f32[2,4,128,128]{3,2,1,0:T(8,128)} copy(f32[2,4,128,128]{3,2,1,0:T(8,128)S(1)} %shard_map.46) | data formatting | bytes 1048576

commit v5 on v3

--- a/solution.py
+++ b/solution.py
@@ -115,6 +115,9 @@
         lax.fori_loop(1, na, functools.partial(step, shifts=[0] + away), 0)
 
     def each_peer_by_plane(visit):
+        trial = lax.axis_index("trial")
+        order = [(1 - trial) * j + trial * places[shift] for j, shift in enumerate(away + [0])]
+
         def step(i, carry, planes):
             pa = lax.rem(a + i, na)
             for pb in planes:
@@ -123,7 +126,7 @@
 
         for j in away:
             visit(a * nb + places[j], {"qa": a, "qb": places[j]})
-        for planes in (range(nb // 2), range(nb // 2, nb)):
+        for planes in (order[: nb // 2], order[nb // 2 :]):
             lax.fori_loop(1, na, functools.partial(step, planes=planes), 0)
 
     fetched = [

time: 61.3 us -> 61.3 us (level)
  no operation moved by 1% of the time
where the time goes in v5:
time: 61.3 us; the launch traced here: 61.2 us
  Pallas kernels  60.4 us (99%)
  local copies, waits for them, and re-layouts  0.8 us (1%)
    pallas_call x1, Pallas kernels, fused(): pl.pallas_call(functools.partial(kernel, na, nb), out_shape=jax.ShapeDtyp...  60.4 us

profile of v5, /device:TPU:8, one launch (start us, length us, event | category | flops | bytes accessed | tf_op | source)
XLA Modules:
  0.0 61.2 jit_solution(18208463141179887156)
XLA Ops:
  0.0 60.4 %shard_map.46 = f32[2,4,128,128]{3,2,1,0:T(8,128)S(1)} custom-call(f32[2,4,128,128]{3,2,1,0:T(8,128)} %wave_hbm.1, f32[4,128,128]{2,1,0:T(8,128)} %level_hbm.1, f32[3,128]{1,0:T(4,128)} %diag_hbm.1, f32[3,4]{1,0:T(4,128)} %turns_hbm.1), custom_call_target="tpu_custom_call" | custom-call | tf_op jit(solution)/shard_map/pallas_call | solution.py:334
  60.5 0.8 %copy.6 = f32[2,4,128,128]{3,2,1,0:T(8,128)} copy(f32[2,4,128,128]{3,2,1,0:T(8,128)S(1)} %shard_map.46) | data formatting | bytes 1048576
